TPU v7x, 128 devices: a whole 4x4x4 slice. The times are simulated.
128 devices in a mesh: dp: 16 (over x_lo, z, core), expert: 8 (over y, x_hi).
Axes of the slice: x: 4 (x_hi: 2, x_lo: 2; x = x_hi * 2 + x_lo), y: 4, z: 4, core: 2. Of those that a mesh axis runs over, the one named last changes fastest.
Arguments:
- tokens: bfloat16 [16384, 2048], P(('dp', 'expert')), may hold values from -6 to 6
- norm_gain: float32 [2048], replicated, may hold values from 0.25 to 1.75
- router_weight: bfloat16 [2048, 64], P('dp'), may hold values from -0.25 to 0.25
- expert_ids: int32 [16384, 8], P(('dp', 'expert')), may hold values from 0 to 63, all different within a row; in each aligned block of 128 rows (0 to 127, 128 to 255, ...) at most 32 rows name the same one
- gate_weight: bfloat16 [8, 2048, 1024], P('expert', 'dp'), may hold values from -0.125 to 0.125
- up_weight: bfloat16 [8, 2048, 1024], P('expert', 'dp'), may hold values from -0.125 to 0.125
- down_weight: bfloat16 [8, 2048, 1024], P('expert', 'dp'), may hold values from -0.1875 to 0.1875
- cotangent: bfloat16 [16384, 2048], P(('dp', 'expert')), may hold values from -6 to 6
Outputs:
- mixed: bfloat16 [16384, 2048], P(('dp', 'expert'))
- d_tokens: bfloat16 [16384, 2048], P(('dp', 'expert'))
- d_gain: float32 [2048], replicated
- d_router: float32 [2048, 64], P('dp')
- d_gate: bfloat16 [8, 2048, 1024], P('expert', 'dp')
- d_up: bfloat16 [8, 2048, 1024], P('expert', 'dp')
- d_down: bfloat16 [8, 2048, 1024], P('expert', 'dp')
Inputs may be any that keep to these rules, and one draw needn't show every extreme that they name: `expert_ids`: each row names 8 different experts; in the rows of one device no expert is named more than 32 times.
All inputs are finite; a program needn't handle non-finite values.
Results may differ from a plain program's by a relative error of at most 0.018.
Values may be sent and summed in bfloat16 or wider, within the bound.
No kernel may reach another device: no remote copies, remote signals or barrier semaphores. Data moves between devices by JAX's collectives and lax.ppermute only.
A program may use at most 128 MiB of HBM per device.

v0:
```python
import jax
import jax.numpy as jnp
from jax import lax
from jax.sharding import PartitionSpec as P

D = 2048
FF = 1024
CAP = 32
EPSILON = 1e-05
HIGHEST = lax.Precision.HIGHEST


def in_one_piece(arrays, axis, dim, along):
    both = jnp.concatenate(arrays, axis=along)
    result, at, finished = (lax.all_gather(both, axis, axis=dim, tiled=True), 0, [])
    for a in arrays:
        finished.append(lax.slice_in_dim(result, at, at + a.shape[along], axis=along))
        at += a.shape[along]
    return tuple(finished)


def split_up(x, dim, length):
    shape = x.shape
    pieces = x.reshape(*shape[:dim], length, shape[dim] // length, *shape[dim + 1 :])
    return jnp.moveaxis(pieces, dim, 0)


def sum_at_owner(x, axis, dim):
    length = lax.axis_size(axis)
    pieces = lax.all_to_all(split_up(x, dim, length), axis, 0, 0, tiled=True)
    return jnp.sum(pieces.astype(jnp.float32), axis=0)


def copy_for_each(x, axis):
    copies = jnp.broadcast_to(x, (lax.axis_size(axis), *x.shape))
    return lax.all_to_all(copies, axis, split_axis=0, concat_axis=0, tiled=True)


def over_copies(x, axis):
    everything = copy_for_each(x, axis)
    return jnp.sum(everything.astype(jnp.float32), axis=0)


def normalize(inputs, norm_gain):
    meansq = jnp.mean(inputs * inputs, axis=-1, keepdims=True)
    return inputs * lax.rsqrt(meansq + EPSILON) * norm_gain


def gate_weights(logits, expert_ids):
    member = (
        expert_ids[:, :, None] == jnp.arange(logits.shape[-1], dtype=jnp.int32)[None, None, :]
    ).astype(jnp.float32)
    picked = jnp.sum(member * logits[:, None, :], axis=-1)
    raised = jnp.exp(picked)
    return raised / jnp.sum(raised, axis=-1, keepdims=True)


def pick_matrix(expert_ids, window, capacity):
    flat_ids = expert_ids.reshape(-1)
    chosen = (flat_ids[:, None] == jnp.arange(window, dtype=jnp.int32)[None, :]).astype(jnp.int32)
    before = jnp.cumsum(chosen, axis=0, dtype=jnp.int32) - chosen
    position = jnp.sum(before * chosen, axis=-1)
    target = jnp.where(flat_ids < window, flat_ids * capacity + position, -1)
    columns = jnp.arange(window * capacity, dtype=jnp.int32)
    matrix = (target[:, None] == columns[None, :]).astype(jnp.float32)
    return matrix.reshape(expert_ids.shape[0], expert_ids.shape[1], window * capacity)


def expert_forward(slot_rows, w_gate, w_up, w_down):
    gate_pre = jnp.dot(slot_rows, w_gate, preferred_element_type=jnp.float32)
    up_pre = jnp.dot(slot_rows, w_up, preferred_element_type=jnp.float32)
    active = (gate_pre * jax.nn.sigmoid(gate_pre) * up_pre).astype(jnp.bfloat16)
    output = jnp.dot(active, w_down.T, preferred_element_type=jnp.float32).astype(jnp.bfloat16)
    return (output, gate_pre, up_pre)


def expert_backward(slot_grads, gate_pre, up_pre, w_gate, w_up, w_down):
    sigmoid_gate = jax.nn.sigmoid(gate_pre)
    active = (gate_pre * sigmoid_gate * up_pre).astype(jnp.bfloat16)
    back = jnp.dot(slot_grads, w_down, preferred_element_type=jnp.float32)
    grad_gate = (back * up_pre * sigmoid_gate * (1.0 + gate_pre * (1.0 - sigmoid_gate))).astype(
        jnp.bfloat16
    )
    grad_upper = (back * gate_pre * sigmoid_gate).astype(jnp.bfloat16)
    grad_rows = jnp.dot(grad_gate, w_gate.T, preferred_element_type=jnp.float32)
    grad_rows = (
        grad_rows + jnp.dot(grad_upper, w_up.T, preferred_element_type=jnp.float32)
    ).astype(jnp.bfloat16)
    return (grad_rows, active, grad_gate, grad_upper)


def body(
    tokens, norm_gain, router_weight, expert_ids, gate_weight, up_weight, down_weight, cotangent
):
    window = lax.axis_size("expert")
    slot_count = window * CAP
    router_full = lax.all_gather(router_weight, "dp", axis=0, tiled=True)
    inputs = tokens.astype(jnp.float32)
    hidden = normalize(inputs, norm_gain).astype(jnp.bfloat16)
    logits = jnp.dot(hidden, router_full, preferred_element_type=jnp.float32)
    weights, gate_back = jax.vjp(lambda values: gate_weights(values, expert_ids), logits)
    pick_table = pick_matrix(expert_ids, window, CAP)
    spread_half = jnp.sum(pick_table, axis=1).astype(jnp.bfloat16)
    blending = jnp.einsum("tks,tk->ts", pick_table, weights, precision=HIGHEST)
    outgoing = (
        jnp.dot(spread_half.T, hidden, preferred_element_type=jnp.float32)
        .astype(jnp.bfloat16)
        .reshape(window, CAP, D)
    )
    weights_full = in_one_piece((gate_weight, up_weight, down_weight), "dp", 1, 0)
    w_gate = weights_full[0][0]
    w_up = weights_full[1][0]
    w_down = weights_full[2][0]
    arrived_rows = lax.all_to_all(outgoing, "expert", split_axis=0, concat_axis=0, tiled=True)
    lead = arrived_rows.shape[0]
    middle = arrived_rows.shape[1]
    output, gate_pre, up_pre = expert_forward(arrived_rows.reshape(-1, D), w_gate, w_up, w_down)
    produced = output.reshape(lead, middle, D)
    gate_slots = gate_pre.reshape(lead, middle, FF)
    upper_slots = up_pre.reshape(lead, middle, FF)
    returned = lax.all_to_all(produced, "expert", split_axis=0, concat_axis=0, tiled=True).reshape(
        slot_count, D
    )
    returned_wide = returned.astype(jnp.float32)
    mixed_out = jnp.dot(blending, returned_wide, precision=HIGHEST).astype(jnp.bfloat16)
    gathered_cot = jnp.dot(spread_half.T, cotangent, preferred_element_type=jnp.float32)
    per_slot = jnp.sum(gathered_cot * returned_wide, axis=-1)
    grad_weights = jnp.einsum("tks,s->tk", pick_table, per_slot, precision=HIGHEST)
    grad_logits = gate_back(grad_weights)[0]
    outgoing_grad = (
        jnp.dot(blending.T, cotangent.astype(jnp.float32), precision=HIGHEST)
        .astype(jnp.bfloat16)
        .reshape(window, CAP, D)
    )
    arrived_grad = lax.all_to_all(outgoing_grad, "expert", split_axis=0, concat_axis=0, tiled=True)
    flat_rows = arrived_rows.reshape(-1, D)
    flat_grads = arrived_grad.reshape(-1, D)
    grad_rows, active, grad_gate, grad_upper = expert_backward(
        flat_grads, gate_slots.reshape(-1, FF), upper_slots.reshape(-1, FF), w_gate, w_up, w_down
    )
    grad_back = lax.all_to_all(
        grad_rows.reshape(window, CAP, D), "expert", split_axis=0, concat_axis=0, tiled=True
    ).reshape(slot_count, D)
    term_gate = jnp.dot(flat_rows.T, grad_gate, preferred_element_type=jnp.float32)
    term_upper = jnp.dot(flat_rows.T, grad_upper, preferred_element_type=jnp.float32)
    term_down = jnp.dot(flat_grads.T, active, preferred_element_type=jnp.float32)
    summed = lax.psum_scatter(
        jnp.concatenate([term_gate, term_upper, term_down], axis=1).astype(jnp.bfloat16),
        "dp",
        scatter_dimension=0,
        tiled=True,
    ).astype(jnp.float32)
    grad_hidden = jnp.dot(spread_half, grad_back, preferred_element_type=jnp.float32)
    grad_hidden = grad_hidden + jnp.dot(
        grad_logits, router_full.astype(jnp.float32).T, precision=HIGHEST
    )
    unused_value, norm_back = jax.vjp(normalize, inputs, norm_gain)
    grad_inputs, grad_gain = norm_back(grad_hidden)
    grad_router = jnp.dot(hidden.astype(jnp.float32).T, grad_logits, precision=HIGHEST)
    router_part = sum_at_owner(grad_router.astype(jnp.bfloat16), "dp", 0)
    router_mine = over_copies(router_part.astype(jnp.bfloat16), "expert").astype(jnp.float32)
    gain_sum = lax.psum(grad_gain, ("dp", "expert"))
    grad_gate_out = summed[:, :FF].astype(jnp.bfloat16)[None]
    grad_up_out = summed[:, FF : 2 * FF].astype(jnp.bfloat16)[None]
    grad_down_out = summed[:, 2 * FF :].astype(jnp.bfloat16)[None]
    return (
        mixed_out,
        grad_inputs.astype(jnp.bfloat16),
        gain_sum,
        router_mine,
        grad_gate_out,
        grad_up_out,
        grad_down_out,
    )


def solution(mesh):
    in_specs = (
        P(("dp", "expert"), None),
        P(),
        P("dp", None),
        P(("dp", "expert"), None),
        P("expert", "dp", None),
        P("expert", "dp", None),
        P("expert", "dp", None),
        P(("dp", "expert"), None),
    )
    out_specs = (
        P(("dp", "expert"), None),
        P(("dp", "expert"), None),
        P(),
        P("dp", None),
        P("expert", "dp", None),
        P("expert", "dp", None),
        P("expert", "dp", None),
    )
    return jax.shard_map(body, mesh=mesh, in_specs=in_specs, out_specs=out_specs, check_vma=False)
```

profile of v0, /device:TPU:1, one launch (start us, length us, event | category | flops | bytes accessed | tf_op | source)
XLA Modules:
  0.0 330.0 jit_solution(3319858266487233548)
XLA Ops:
  7.3 2.2 pad_maximum_fusion.1
  10.4 2.3 reduce-window.6
  15.9 2.5 convolution_convert_fusion.3
  18.4 7.5 %all-to-all-start = ((bf16[8,32,2048]{2,1,0:T(8,128)(2,1)}), bf16[8,32,2048]{2,1,0:T(8,128)(2,1)S(1)}, u32[]{:S(2)}, u32[]{:S(2)}) async-start(bf16[8,32,2048]{2,1,0:T(8,128)(2,1)} %bitcast.3), calls=%async_computation | async-start | bytes 2097152 | tf_op jit(solution)/shard_map/all_to_all | solution.py:114
  25.9 41.0 %all_gather.6 = bf16[2048,64]{0,1:T(8,128)(2,1)S(1)} all-gather(bf16[128,64]{0,1:T(8,128)(2,1)S(1)} %copy-done.14), channel_id=1, replica_groups=mesh['dp'=16,'expert'=8] {'dp'}, dimensions={0}, use_global_device_ids=true | all-gather | bytes 278528 | tf_op jit(solution)/shard_map/all_gather | solution.py:97
  71.1 6.8 %all-to-all-start.2 = ((bf16[8,32,2048]{2,1,0:T(8,128)(2,1)}), bf16[8,32,2048]{2,1,0:T(8,128)(2,1)S(1)}, u32[]{:S(2)}, u32[]{:S(2)}) async-start(bf16[8,32,2048]{2,1,0:T(8,128)(2,1)} %bitcast.109), calls=%async_computation.2 | async-start | bytes 2097152 | tf_op jit(solution)/shard_map/all_to_all | solution.py:135
  78.1 30.4 %all-gather.2.cloned.1.call-done = bf16[3,2048,1024]{2,1,0:T(8,128)(2,1)} async-done(((bf16[3,128,1024]{2,1,0:T(8,128)(2,1)}), bf16[3,2048,1024]{2,1,0:T(8,128)(2,1)}) %all-gather.2.cloned.1.call-update) | async-done | bytes 12582928 | tf_op jit(solution)/shard_map/all_gather | solution.py:15
  108.5 4.4 %fusion.3 = f32[256,1024]{1,0:T(8,128)} fusion(bf16[256,2048]{1,0:T(8,128)(2,1)S(1)} %bitcast.100, bf16[3,2048,1024]{2,1,0:T(8,128)(2,1)} %all-gather.2.cloned.1.call-done), kind=kOutput, calls=%fused_computation.10 | convolution fusion | flops 1073741824 | bytes 6291456 | tf_op jit(solution)/shard_map/dot_general | solution.py:71
  112.9 4.4 %fusion.1 = f32[256,1024]{1,0:T(8,128)} fusion(bf16[256,2048]{1,0:T(8,128)(2,1)S(1)} %bitcast.101, bf16[3,2048,1024]{2,1,0:T(8,128)(2,1)} %all-gather.2.cloned.1.call-done), kind=kOutput, calls=%fused_computation.8 | convolution fusion | flops 1073741824 | bytes 6291456 | tf_op jit(solution)/shard_map/dot_general | solution.py:70
  117.3 4.4 %multiply_convert_fusion = (bf16[256,1024]{1,0:T(8,128)(2,1)S(1)}, bf16[256,1024]{1,0:T(8,128)(2,1)S(1)}, bf16[256,1024]{1,0:T(8,128)(2,1)S(1)}) fusion(f32[256,1024]{1,0:T(8,128)} %fusion.1, f32[256,1024]{1,0:T(8,128)} %fusion.3, bf16[256,2048]{1,0:T(8,128)(2,1)S(1)} %bitcast.104, bf16[3,2048,1024]{2,1,0:T(8,128)(2,1)} %all-gather.2.cloned.1.call-done), kind=kOutput, calls=%fused_computation.36 | convolution fusion | flops 1077936128 | bytes 8912896 | tf_op jit(solution)/shard_map/dot_general | solution.py:80
  125.7 21.2 %pad_maximum_fusion = bf16[2048,3072]{0,1:T(8,128)(2,1)} fusion(bf16[2048,1024]{0,1:T(8,128)(2,1)S(1)} %convolution_convert_fusion, bf16[2048,1024]{0,1:T(8,128)(2,1)S(1)} %convolution_convert_fusion.1, bf16[2048,1024]{0,1:T(8,128)(2,1)S(1)} %convolution_convert_fusion.2), kind=kLoop, calls=%fused_computation | loop fusion | flops 37748736 | bytes 25165824 | tf_op jit(solution)/shard_map/concatenate | solution.py:148
  146.9 16.6 %copy.68 = bf16[2048,3072]{1,0:T(8,128)(2,1)} copy(bf16[2048,3072]{0,1:T(8,128)(2,1)} %pad_maximum_fusion) | data formatting | bytes 25165824
  164.6 4.6 %fusion.8 = bf16[256,2048]{1,0:T(8,128)(2,1)} fusion(bf16[256,1024]{1,0:T(8,128)(2,1)S(1)} %copy-done.8, bf16[3,2048,1024]{2,1,0:T(8,128)(2,1)} %all-gather.2.cloned.1.call-done), kind=kOutput, calls=%fused_computation.17 | convolution fusion | flops 1074266112 | bytes 5767168 | tf_op jit(solution)/shard_map/dot_general | solution.py:73
  169.2 6.1 %all-to-all-start.1 = ((bf16[8,32,2048]{2,1,0:T(8,128)(2,1)}), bf16[8,32,2048]{2,1,0:T(8,128)(2,1)S(1)}, u32[]{:S(2)}, u32[]{:S(2)}) async-start(bf16[8,32,2048]{2,1,0:T(8,128)(2,1)} %bitcast.8), calls=%async_computation.1 | async-start | bytes 2097152 | tf_op jit(solution)/shard_map/all_to_all | solution.py:121
  175.3 3.5 %fusion = f32[256,2048]{1,0:T(8,128)S(1)} fusion(bf16[256,1024]{1,0:T(8,128)(2,1)S(1)} %copy-done.6, bf16[3,2048,1024]{2,1,0:T(8,128)(2,1)} %all-gather.2.cloned.1.call-done), kind=kOutput, calls=%fused_computation.7 | convolution fusion | flops 1073741824 | bytes 6815744 | tf_op jit(solution)/shard_map/dot_general | solution.py:85
  178.9 4.5 %fusion.7 = bf16[256,2048]{1,0:T(8,128)(2,1)} fusion(f32[256,2048]{1,0:T(8,128)S(1)} %fusion, bf16[256,1024]{1,0:T(8,128)(2,1)S(1)} %copy-done.4, bf16[3,2048,1024]{2,1,0:T(8,128)(2,1)} %all-gather.2.cloned.1.call-done), kind=kOutput, calls=%fused_computation.16 | convolution fusion | flops 1074790400 | bytes 7864320 | tf_op jit(solution)/shard_map/dot_general | solution.py:87
  183.4 14.9 %all-to-all-done.1 = bf16[8,32,2048]{2,1,0:T(8,128)(2,1)S(1)} async-done(((bf16[8,32,2048]{2,1,0:T(8,128)(2,1)}), bf16[8,32,2048]{2,1,0:T(8,128)(2,1)S(1)}, u32[]{:S(2)}, u32[]{:S(2)}) %all-to-all-start.1) | async-done | bytes 1048608 | tf_op jit(solution)/shard_map/all_to_all | solution.py:121
  198.3 3.6 %all-to-all-start.3 = ((bf16[8,32,2048]{2,1,0:T(8,128)(2,1)}), bf16[8,32,2048]{2,1,0:T(8,128)(2,1)S(1)}, u32[]{:S(2)}, u32[]{:S(2)}) async-start(bf16[8,32,2048]{2,1,0:T(8,128)(2,1)} %bitcast.110), calls=%async_computation.3 | async-start | bytes 2097152 | tf_op jit(solution)/shard_map/all_to_all | solution.py:141
  202.4 3.6 %fusion.18 = f32[1,128,8]{2,0,1:T(1,128)S(1)} fusion(f32[256,1,1]{0,1,2:T(1,128)S(1)} %bitcast.115, s32[128,8]{1,0:T(8,128)S(1)} %copy.59), kind=kOutput, calls=%fused_computation.42 | convolution fusion | flops 3407872 | bytes 9216 | tf_op jit(solution)/shard_map/tks,s->tk/dot_general | solution.py:128
  207.6 16.8 %all-to-all-done.3 = bf16[8,32,2048]{2,1,0:T(8,128)(2,1)S(1)} async-done(((bf16[8,32,2048]{2,1,0:T(8,128)(2,1)}), bf16[8,32,2048]{2,1,0:T(8,128)(2,1)S(1)}, u32[]{:S(2)}, u32[]{:S(2)}) %all-to-all-start.3) | async-done | bytes 1048608 | tf_op jit(solution)/shard_map/all_to_all | solution.py:141
  224.4 6.8 %all-to-all-start.4 = ((bf16[16,128,64]{1,2,0:T(8,128)(2,1)}), bf16[16,128,64]{1,2,0:T(8,128)(2,1)S(1)}, u32[]{:S(2)}, u32[]{:S(2)}) async-start(bf16[16,128,64]{1,2,0:T(8,128)(2,1)} %bitcast.98), calls=%async_computation.4 | async-start | bytes 524288 | tf_op jit(solution)/shard_map/all_to_all | solution.py:30
  235.2 5.1 %all-to-all-done.4 = bf16[16,128,64]{1,2,0:T(8,128)(2,1)S(1)} async-done(((bf16[16,128,64]{1,2,0:T(8,128)(2,1)}), bf16[16,128,64]{1,2,0:T(8,128)(2,1)S(1)}, u32[]{:S(2)}, u32[]{:S(2)}) %all-to-all-start.4) | async-done | bytes 262176 | tf_op jit(solution)/shard_map/all_to_all | solution.py:30
  241.0 3.4 %all-to-all-start.5 = ((bf16[8,128,64]{1,2,0:T(8,128)(2,1)}), bf16[8,128,64]{1,2,0:T(8,128)(2,1)S(1)}, u32[]{:S(2)}, u32[]{:S(2)}) async-start(bf16[8,128,64]{1,2,0:T(8,128)(2,1)} %broadcast_in_dim.44), calls=%async_computation.5 | async-start | bytes 262144 | tf_op jit(solution)/shard_map/all_to_all | solution.py:36
  245.8 72.5 %psum.7 = f32[2048]{0:T(1024)} all-reduce(f32[2048]{0:T(1024)S(1)} %get-tuple-element.42), channel_id=1, replica_groups=mesh['dp'=16,'expert'=8] {'dp','expert'}, use_global_device_ids=true, to_apply=%region_12.13 | all-reduce | flops 2048 | bytes 16384 | tf_op jit(solution)/shard_map/psum | solution.py:162
  (93 shorter events, 26.4 us)
Async XLA Ops:
  7.2 61.8 %copy-start = (bf16[128,2048]{1,0:T(8,128)(2,1)S(1)}, bf16[128,2048]{1,0:T(8,128)(2,1)}, u32[]{:S(2)}) copy-start(bf16[128,2048]{1,0:T(8,128)(2,1)} %param.15) | copy-start | bytes 1572868
  7.2 60.9 %copy-start.13 = (s32[128,8]{0,1:T(8,128)S(1)}, s32[128,8]{0,1:T(8,128)}, u32[]{:S(2)}) copy-start(s32[128,8]{0,1:T(8,128)} %param.11) | copy-start | bytes 12292
  7.2 60.5 %copy-start.1 = (bf16[128,2048]{1,0:T(8,128)(2,1)S(1)}, bf16[128,2048]{1,0:T(8,128)(2,1)}, u32[]{:S(2)}) copy-start(bf16[128,2048]{1,0:T(8,128)(2,1)} %param.8) | copy-start | bytes 1572868
  7.2 60.5 %copy-start.12 = (f32[2048]{0:T(1024)S(1)}, f32[2048]{0:T(1024)}, u32[]{:S(2)}) copy-start(f32[2048]{0:T(1024)} %param.9) | copy-start | bytes 24580
  7.2 18.7 %copy-start.14 = (bf16[128,64]{0,1:T(8,128)(2,1)S(1)}, bf16[128,64]{0,1:T(8,128)(2,1)}, u32[]{:S(2)}) copy-start(bf16[128,64]{0,1:T(8,128)(2,1)} %param.10) | copy-start | bytes 49156
  7.2 101.3 %all-gather.2.cloned.1.call-start = ((), (), s32[]{:S(2)}) async-start(), calls=%async_computation.7 | async-start | bytes 13369344 | tf_op jit(solution)/shard_map/all_gather | solution.py:15
  15.9 10.0 %copy-start.17 = (f32[128]{0:T(128)}, f32[128]{0:T(128)S(1)}, u32[]{:S(2)}) copy-start(f32[128]{0:T(128)S(1)} %fusion.16) | copy-start | bytes 1540
  15.9 190.3 %copy-start.15 = (f32[128]{0:T(128)}, f32[128]{0:T(128)S(1)}, u32[]{:S(2)}) copy-start(f32[128]{0:T(128)S(1)} %fusion.34) | copy-start | bytes 1540
  18.4 52.6 %all-to-all-start = ((bf16[8,32,2048]{2,1,0:T(8,128)(2,1)}), bf16[8,32,2048]{2,1,0:T(8,128)(2,1)S(1)}, u32[]{:S(2)}, u32[]{:S(2)}) async-start(bf16[8,32,2048]{2,1,0:T(8,128)(2,1)} %bitcast.3), calls=%async_computation | async-start | bytes 2097152 | tf_op jit(solution)/shard_map/all_to_all | solution.py:114
  69.0 2.1 copy-start.9
  71.1 46.3 %all-to-all-start.2 = ((bf16[8,32,2048]{2,1,0:T(8,128)(2,1)}), bf16[8,32,2048]{2,1,0:T(8,128)(2,1)S(1)}, u32[]{:S(2)}, u32[]{:S(2)}) async-start(bf16[8,32,2048]{2,1,0:T(8,128)(2,1)} %bitcast.109), calls=%async_computation.2 | async-start | bytes 2097152 | tf_op jit(solution)/shard_map/all_to_all | solution.py:135
  77.9 241.0 %reduce-scatter.4.cloned.1.call-start = ((), (), s32[]{:S(2)}) async-start(), calls=%async_computation.8 | async-start | bytes 13369344
  121.7 1.4 copy-start.7
  121.7 1.4 copy-start.3
  121.7 2.7 copy-start.5
  163.5 1.0 copy-start.8
  164.6 10.7 %copy-start.6 = (bf16[256,1024]{1,0:T(8,128)(2,1)S(1)}, bf16[256,1024]{1,0:T(8,128)(2,1)}, u32[]{:S(2)}) copy-start(bf16[256,1024]{1,0:T(8,128)(2,1)} %copy-done.5) | copy-start | bytes 1572868
  169.2 29.1 %all-to-all-start.1 = ((bf16[8,32,2048]{2,1,0:T(8,128)(2,1)}), bf16[8,32,2048]{2,1,0:T(8,128)(2,1)S(1)}, u32[]{:S(2)}, u32[]{:S(2)}) async-start(bf16[8,32,2048]{2,1,0:T(8,128)(2,1)} %bitcast.8), calls=%async_computation.1 | async-start | bytes 2097152 | tf_op jit(solution)/shard_map/all_to_all | solution.py:121
  175.3 3.5 %copy-start.4 = (bf16[256,1024]{1,0:T(8,128)(2,1)S(1)}, bf16[256,1024]{1,0:T(8,128)(2,1)}, u32[]{:S(2)}) copy-start(bf16[256,1024]{1,0:T(8,128)(2,1)} %copy-done.3) | copy-start | bytes 1572868
  198.3 26.1 %all-to-all-start.3 = ((bf16[8,32,2048]{2,1,0:T(8,128)(2,1)}), bf16[8,32,2048]{2,1,0:T(8,128)(2,1)S(1)}, u32[]{:S(2)}, u32[]{:S(2)}) async-start(bf16[8,32,2048]{2,1,0:T(8,128)(2,1)} %bitcast.110), calls=%async_computation.3 | async-start | bytes 2097152 | tf_op jit(solution)/shard_map/all_to_all | solution.py:141
  224.4 15.9 %all-to-all-start.4 = ((bf16[16,128,64]{1,2,0:T(8,128)(2,1)}), bf16[16,128,64]{1,2,0:T(8,128)(2,1)S(1)}, u32[]{:S(2)}, u32[]{:S(2)}) async-start(bf16[16,128,64]{1,2,0:T(8,128)(2,1)} %bitcast.98), calls=%async_computation.4 | async-start | bytes 524288 | tf_op jit(solution)/shard_map/all_to_all | solution.py:30
  231.2 2.9 copy-start.16
  231.5 12.9 %copy-start.10 = (f32[128,1,256]{2,1,0:T(1,128)S(1)}, f32[128,1,256]{2,1,0:T(1,128)}, u32[]{:S(2)}) copy-start(f32[128,1,256]{2,1,0:T(1,128)} %copy-done.9) | copy-start | bytes 393220
  241.0 77.3 %all-to-all-start.5 = ((bf16[8,128,64]{1,2,0:T(8,128)(2,1)}), bf16[8,128,64]{1,2,0:T(8,128)(2,1)S(1)}, u32[]{:S(2)}, u32[]{:S(2)}) async-start(bf16[8,128,64]{1,2,0:T(8,128)(2,1)} %broadcast_in_dim.44), calls=%async_computation.5 | async-start | bytes 262144 | tf_op jit(solution)/shard_map/all_to_all | solution.py:36
  (2 other events, 1.3 us)
Sparse Core Ops, SparseCore 0:
  9.7 98.7 all-gather.1
  163.7 106.8 reduce-scatter.3
where the time goes:
time: 331 us; the launch traced here: 330 us
  blocking collectives  114 us (34%)
  waiting for transfers between devices  67.2 us (20%)
  matrix products  43.8 us (13%)
  starting transfers between devices  34.4 us (10%)
  other arithmetic  30.8 us (9%)
  local copies, waits for them, and re-layouts  25.9 us (8%)
  between operations  14.4 us (4%)
    psum x1, blocking collectives, body(): gain_sum = lax.psum(grad_gain, ('dp', 'expert'))  72.5 us
    all_gather x1, blocking collectives, body(): router_full = lax.all_gather(router_weight, 'dp', axis=0, tiled=True)  41 us
    all_gather x1, waiting for transfers between devices, in_one_piece(): lax.all_gather(both, axis, axis=dim, tiled=True)  30.4 us
    unnamed x44, local copies, waits for them, and re-layouts  22.4 us
    concatenate x1, other arithmetic, body(): jnp.concatenate([term_gate, term_upper, term_down], axis=1)  21.2 us
    all_to_all x1, waiting for transfers between devices, body(): lax.all_to_all(grad_rows.reshape(window, CAP, D), 'expert', split_axis=0,...  16.8 us
    all_to_all x1, waiting for transfers between devices, body(): lax.all_to_all(produced, 'expert', split_axis=0, concat_axis=0, tiled=True)  14.9 us
    all_to_all x1, starting transfers between devices, body(): lax.all_to_all(outgoing, 'expert', split_axis=0, concat_axis=0, tiled=True)  7.46 us
  transfers between devices with their start and end apart: 8, of which 4 were waited for; matrix products, arithmetic and copies ran while one was open for 14% of the time, Pallas kernels for 0%

commit v1 on v0

--- a/solution.py
+++ b/solution.py
@@ -159,7 +159,7 @@
     grad_router = jnp.dot(hidden.astype(jnp.float32).T, grad_logits, precision=HIGHEST)
     router_part = sum_at_owner(grad_router.astype(jnp.bfloat16), "dp", 0)
     router_mine = over_copies(router_part.astype(jnp.bfloat16), "expert").astype(jnp.float32)
-    gain_sum = lax.psum(grad_gain, ("dp", "expert"))
+    gain_sum = jnp.sum(lax.all_gather(grad_gain, ("dp", "expert")), axis=0)
     grad_gate_out = summed[:, :FF].astype(jnp.bfloat16)[None]
     grad_up_out = summed[:, FF : 2 * FF].astype(jnp.bfloat16)[None]
     grad_down_out = summed[:, 2 * FF :].astype(jnp.bfloat16)[None]

time: 331 us -> 573 us (1.73)
  waiting for transfers between devices: 67.2 us -> 366 us
  blocking collectives: 114 us -> 41 us
  matrix products: 43.8 us -> 50.2 us
    all_gather x0 -> x1, waiting for transfers between devices: none -> 231 us  [body(): gain_sum = jnp.sum(lax.all_gather(grad_gain, ('dp', 'expert')), axis=0)]
    unnamed x3 -> x4, waiting for transfers between devices: 0.03 us -> 79.8 us
    psum x1 -> x0, blocking collectives: 72.5 us -> none  [body(): gain_sum = lax.psum(grad_gain, ('dp', 'expert'))]
    all_to_all x1, waiting for transfers between devices: 16.8 us -> 5.84 us  [body(): lax.all_to_all(grad_rows.reshape(window, CAP, D), 'expert', split_axis=0,...]
    all_to_all x1, waiting for transfers between devices: 14.9 us -> 8.7 us  [body(): lax.all_to_all(produced, 'expert', split_axis=0, concat_axis=0, tiled=True)]
    unnamed x44 -> x46, local copies, waits for them, and re-layouts: 22.4 us -> 22.5 us
  transfers between devices with their start and end apart: 8 -> 9, of which waited for: 4 -> 7; matrix products, arithmetic and copies ran while one was open for 14% -> 16% of each run, Pallas kernels for 0% -> 0%
where the time goes in v1:
time: 573 us; the launch traced here: 569 us
  waiting for transfers between devices  366 us (64%)
  matrix products  50.2 us (9%)
  blocking collectives  41 us (7%)
  starting transfers between devices  35.7 us (6%)
  other arithmetic  33.3 us (6%)
  local copies, waits for them, and re-layouts  28.1 us (5%)
  between operations  14.1 us (2%)
    all_gather x1, waiting for transfers between devices, body(): gain_sum = jnp.sum(lax.all_gather(grad_gain, ('dp', 'expert')), axis=0)  231 us
    unnamed x4, waiting for transfers between devices  79.8 us
    all_gather x1, blocking collectives, body(): router_full = lax.all_gather(router_weight, 'dp', axis=0, tiled=True)  41 us
    all_gather x1, waiting for transfers between devices, in_one_piece(): lax.all_gather(both, axis, axis=dim, tiled=True)  30.8 us
    unnamed x46, local copies, waits for them, and re-layouts  22.5 us
    concatenate x1, other arithmetic, body(): jnp.concatenate([term_gate, term_upper, term_down], axis=1)  21.1 us
  transfers between devices with their start and end apart: 9, of which 7 were waited for; matrix products, arithmetic and copies ran while one was open for 16% of the time, Pallas kernels for 0%

profile of v1, /device:TPU:1, one launch (start us, length us, event | category | flops | bytes accessed | tf_op | source)
XLA Modules:
  0.0 568.6 jit_solution(4727913301268692788)
XLA Ops:
  18.4 7.5 %all-to-all-start = ((bf16[8,32,2048]{2,1,0:T(8,128)(2,1)}), bf16[8,32,2048]{2,1,0:T(8,128)(2,1)S(1)}, u32[]{:S(2)}, u32[]{:S(2)}) async-start(bf16[8,32,2048]{2,1,0:T(8,128)(2,1)} %bitcast.3), calls=%async_computation | async-start | bytes 2097152 | tf_op jit(solution)/shard_map/all_to_all | solution.py:114
  25.9 41.0 %all_gather.10 = bf16[2048,64]{0,1:T(8,128)(2,1)S(1)} all-gather(bf16[128,64]{0,1:T(8,128)(2,1)S(1)} %copy-done.13), channel_id=1, replica_groups=mesh['dp'=16,'expert'=8] {'dp'}, dimensions={0}, use_global_device_ids=true | all-gather | bytes 278528 | tf_op jit(solution)/shard_map/all_gather | solution.py:97
  70.8 6.8 %all-to-all-start.2 = ((bf16[8,32,2048]{2,1,0:T(8,128)(2,1)}), bf16[8,32,2048]{2,1,0:T(8,128)(2,1)S(1)}, u32[]{:S(2)}, u32[]{:S(2)}) async-start(bf16[8,32,2048]{2,1,0:T(8,128)(2,1)} %bitcast.106), calls=%async_computation.2 | async-start | bytes 2097152 | tf_op jit(solution)/shard_map/all_to_all | solution.py:135
  77.7 30.8 %all-gather.4.cloned.1.call-done = bf16[3,2048,1024]{2,1,0:T(8,128)(2,1)} async-done(((bf16[3,128,1024]{2,1,0:T(8,128)(2,1)}), bf16[3,2048,1024]{2,1,0:T(8,128)(2,1)}) %all-gather.4.cloned.1.call-update) | async-done | bytes 12582928 | tf_op jit(solution)/shard_map/all_gather | solution.py:15
  108.5 4.4 fusion.3
  112.9 4.4 fusion.1
  117.3 5.3 multiply_convert_fusion
  123.4 4.5 fusion.8
  128.0 6.1 %all-to-all-start.1 = ((bf16[8,32,2048]{2,1,0:T(8,128)(2,1)}), bf16[8,32,2048]{2,1,0:T(8,128)(2,1)}, u32[]{:S(2)}, u32[]{:S(2)}) async-start(bf16[8,32,2048]{2,1,0:T(8,128)(2,1)} %bitcast.108), calls=%async_computation.1 | async-start | bytes 2097152 | tf_op jit(solution)/shard_map/all_to_all | solution.py:121
  134.1 3.7 fusion
  137.8 4.5 fusion.7
  142.3 8.7 %all-to-all-done.1 = bf16[8,32,2048]{2,1,0:T(8,128)(2,1)} async-done(((bf16[8,32,2048]{2,1,0:T(8,128)(2,1)}), bf16[8,32,2048]{2,1,0:T(8,128)(2,1)}, u32[]{:S(2)}, u32[]{:S(2)}) %all-to-all-start.1) | async-done | bytes 1048608 | tf_op jit(solution)/shard_map/all_to_all | solution.py:121
  151.0 4.2 all-to-all-start.3
  158.4 4.3 fusion.18
  164.9 5.8 %all-to-all-done.3 = bf16[8,32,2048]{2,1,0:T(8,128)(2,1)} async-done(((bf16[8,32,2048]{2,1,0:T(8,128)(2,1)}), bf16[8,32,2048]{2,1,0:T(8,128)(2,1)}, u32[]{:S(2)}, u32[]{:S(2)}) %all-to-all-start.3) | async-done | bytes 1048608 | tf_op jit(solution)/shard_map/all_to_all | solution.py:141
  172.3 3.1 fusion.14
  179.5 21.1 %pad_maximum_fusion = bf16[2048,3072]{0,1:T(8,128)(2,1)} fusion(bf16[2048,1024]{0,1:T(8,128)(2,1)S(1)} %convolution_convert_fusion, bf16[2048,1024]{0,1:T(8,128)(2,1)S(1)} %convolution_convert_fusion.1, bf16[2048,1024]{0,1:T(8,128)(2,1)S(1)} %convolution_convert_fusion.2), kind=kLoop, calls=%fused_computation | loop fusion | flops 37748736 | bytes 25165824 | tf_op jit(solution)/shard_map/concatenate | solution.py:148
  200.6 16.6 %copy.68 = bf16[2048,3072]{1,0:T(8,128)(2,1)} copy(bf16[2048,3072]{0,1:T(8,128)(2,1)} %pad_maximum_fusion) | data formatting | bytes 25165824
  219.1 7.3 %all-to-all-start.4 = ((bf16[16,128,64]{1,2,0:T(8,128)(2,1)}), bf16[16,128,64]{1,2,0:T(8,128)(2,1)S(1)}, u32[]{:S(2)}, u32[]{:S(2)}) async-start(bf16[16,128,64]{1,2,0:T(8,128)(2,1)} %bitcast.98), calls=%async_computation.4 | async-start | bytes 524288 | tf_op jit(solution)/shard_map/all_to_all | solution.py:30
  227.6 6.1 %all-to-all-done.4 = bf16[16,128,64]{1,2,0:T(8,128)(2,1)S(1)} async-done(((bf16[16,128,64]{1,2,0:T(8,128)(2,1)}), bf16[16,128,64]{1,2,0:T(8,128)(2,1)S(1)}, u32[]{:S(2)}, u32[]{:S(2)}) %all-to-all-start.4) | async-done | bytes 262176 | tf_op jit(solution)/shard_map/all_to_all | solution.py:30
  234.4 3.4 all-to-all-start.5
  240.5 4.3 all-to-all-done.5
  245.4 230.7 %all-gather.6.cloned.1.call-done = f32[262144]{0:T(1024)} async-done(((f32[2048]{0:T(1024)}), f32[262144]{0:T(1024)}) %all-gather.6.cloned.1.call-update) | async-done | bytes 1048592 | tf_op jit(solution)/shard_map/all_gather | solution.py:162
  478.1 79.8 %reduce-scatter.4.cloned.1.call-done = bf16[128,3072]{1,0:T(8,128)(2,1)} async-done(((bf16[2048,3072]{1,0:T(8,128)(2,1)}), bf16[128,3072]{1,0:T(8,128)(2,1)}) %reduce-scatter.4.cloned.1.call-update) | async-done | bytes 786448
  (99 shorter events, 40.0 us)
Async XLA Ops:
  7.2 61.6 %copy-start = (bf16[128,2048]{1,0:T(8,128)(2,1)S(1)}, bf16[128,2048]{1,0:T(8,128)(2,1)}, u32[]{:S(2)}) copy-start(bf16[128,2048]{1,0:T(8,128)(2,1)} %param.15) | copy-start | bytes 1572868
  7.2 60.2 %copy-start.12 = (s32[128,8]{0,1:T(8,128)S(1)}, s32[128,8]{0,1:T(8,128)}, u32[]{:S(2)}) copy-start(s32[128,8]{0,1:T(8,128)} %param.11) | copy-start | bytes 12292
  7.2 59.8 %copy-start.2 = (bf16[128,2048]{1,0:T(8,128)(2,1)S(1)}, bf16[128,2048]{1,0:T(8,128)(2,1)}, u32[]{:S(2)}) copy-start(bf16[128,2048]{1,0:T(8,128)(2,1)} %param.8) | copy-start | bytes 1572868
  7.2 59.8 %copy-start.11 = (f32[2048]{0:T(1024)S(1)}, f32[2048]{0:T(1024)}, u32[]{:S(2)}) copy-start(f32[2048]{0:T(1024)} %param.9) | copy-start | bytes 24580
  7.2 18.7 %copy-start.13 = (bf16[128,64]{0,1:T(8,128)(2,1)S(1)}, bf16[128,64]{0,1:T(8,128)(2,1)}, u32[]{:S(2)}) copy-start(bf16[128,64]{0,1:T(8,128)(2,1)} %param.10) | copy-start | bytes 49156
  7.2 101.3 %all-gather.4.cloned.1.call-start = ((), (), s32[]{:S(2)}) async-start(), calls=%async_computation.7 | async-start | bytes 13369344 | tf_op jit(solution)/shard_map/all_gather | solution.py:15
  15.9 10.0 %copy-start.17 = (f32[128]{0:T(128)}, f32[128]{0:T(128)S(1)}, u32[]{:S(2)}) copy-start(f32[128]{0:T(128)S(1)} %fusion.16) | copy-start | bytes 1540
  15.9 51.1 %copy-start.15 = (f32[128]{0:T(128)}, f32[128]{0:T(128)S(1)}, u32[]{:S(2)}) copy-start(f32[128]{0:T(128)S(1)} %fusion.34) | copy-start | bytes 1540
  18.4 52.4 %all-to-all-start = ((bf16[8,32,2048]{2,1,0:T(8,128)(2,1)}), bf16[8,32,2048]{2,1,0:T(8,128)(2,1)S(1)}, u32[]{:S(2)}, u32[]{:S(2)}) async-start(bf16[8,32,2048]{2,1,0:T(8,128)(2,1)} %bitcast.3), calls=%async_computation | async-start | bytes 2097152 | tf_op jit(solution)/shard_map/all_to_all | solution.py:114
  68.7 2.1 copy-start.9
  70.8 46.5 %all-to-all-start.2 = ((bf16[8,32,2048]{2,1,0:T(8,128)(2,1)}), bf16[8,32,2048]{2,1,0:T(8,128)(2,1)S(1)}, u32[]{:S(2)}, u32[]{:S(2)}) async-start(bf16[8,32,2048]{2,1,0:T(8,128)(2,1)} %bitcast.106), calls=%async_computation.2 | async-start | bytes 2097152 | tf_op jit(solution)/shard_map/all_to_all | solution.py:135
  128.0 23.0 %all-to-all-start.1 = ((bf16[8,32,2048]{2,1,0:T(8,128)(2,1)}), bf16[8,32,2048]{2,1,0:T(8,128)(2,1)}, u32[]{:S(2)}, u32[]{:S(2)}) async-start(bf16[8,32,2048]{2,1,0:T(8,128)(2,1)} %bitcast.108), calls=%async_computation.1 | async-start | bytes 2097152 | tf_op jit(solution)/shard_map/all_to_all | solution.py:121
  134.1 3.7 copy-start.5
  151.0 19.8 %all-to-all-start.3 = ((bf16[8,32,2048]{2,1,0:T(8,128)(2,1)}), bf16[8,32,2048]{2,1,0:T(8,128)(2,1)}, u32[]{:S(2)}, u32[]{:S(2)}) async-start(bf16[8,32,2048]{2,1,0:T(8,128)(2,1)} %bitcast.107), calls=%async_computation.3 | async-start | bytes 2097152 | tf_op jit(solution)/shard_map/all_to_all | solution.py:141
  155.2 320.8 %all-gather.6.cloned.1.call-start = ((), (), s32[]{:S(2)}) async-start(), calls=%async_computation.8 | async-start | bytes 1056768 | tf_op jit(solution)/shard_map/all_gather | solution.py:162
  158.4 17.1 %copy-start.8 = (bf16[256,1024]{1,0:T(8,128)(2,1)S(1)}, bf16[256,1024]{1,0:T(8,128)(2,1)}, u32[]{:S(2)}) copy-start(bf16[256,1024]{1,0:T(8,128)(2,1)} %copy-done.7) | copy-start | bytes 1572868
  175.4 382.4 %reduce-scatter.4.cloned.1.call-start = ((), (), s32[]{:S(2)}) async-start(), calls=%async_computation.9 | async-start | bytes 13369344
  176.8 1.3 copy-start.4
  217.2 9.3 %copy-start.18 = (f32[128]{0:T(128)S(1)}, f32[128]{0:T(128)}, u32[]{:S(2)}) copy-start(f32[128]{0:T(128)} %copy-done.17) | copy-start | bytes 1540
  217.2 9.3 %copy-start.3 = (f32[128,2048]{1,0:T(8,128)S(1)}, f32[128,2048]{1,0:T(8,128)}, u32[]{:S(2)}) copy-start(f32[128,2048]{1,0:T(8,128)} %get-tuple-element.50) | copy-start | bytes 3145732
  217.9 19.9 %copy-start.10 = (f32[128,1,256]{2,1,0:T(1,128)S(1)}, f32[128,1,256]{2,1,0:T(1,128)}, u32[]{:S(2)}) copy-start(f32[128,1,256]{2,1,0:T(1,128)} %copy-done.9) | copy-start | bytes 393220
  219.1 14.5 %all-to-all-start.4 = ((bf16[16,128,64]{1,2,0:T(8,128)(2,1)}), bf16[16,128,64]{1,2,0:T(8,128)(2,1)S(1)}, u32[]{:S(2)}, u32[]{:S(2)}) async-start(bf16[16,128,64]{1,2,0:T(8,128)(2,1)} %bitcast.98), calls=%async_computation.4 | async-start | bytes 524288 | tf_op jit(solution)/shard_map/all_to_all | solution.py:30
  234.4 10.4 %all-to-all-start.5 = ((bf16[8,128,64]{1,2,0:T(8,128)(2,1)}), bf16[8,128,64]{1,2,0:T(8,128)(2,1)S(1)}, u32[]{:S(2)}, u32[]{:S(2)}) async-start(bf16[8,128,64]{1,2,0:T(8,128)(2,1)} %broadcast_in_dim.44), calls=%async_computation.5 | async-start | bytes 262144 | tf_op jit(solution)/shard_map/all_to_all | solution.py:36
  237.8 324.3 %copy-start.1 = (bf16[128,2048]{1,0:T(8,128)(2,1)S(1)}, bf16[128,2048]{1,0:T(8,128)(2,1)}, u32[]{:S(2)}) copy-start(bf16[128,2048]{1,0:T(8,128)(2,1)} %param.15) | copy-start | bytes 1572868
  (4 other events, 3.3 us)
Sparse Core Ops, SparseCore 0:
  9.7 98.7 all-gather.3
  175.6 300.4 all-gather.5
  478.5 79.3 reduce-scatter.3
